TPU v7x, 128 devices: a whole 4x4x4 slice. The times are simulated.
128 devices in a mesh: row: 8 (over x_lo, z), col: 16 (over x_hi, y, core).
Axes of the slice: x: 4 (x_hi: 2, x_lo: 2; x = x_hi * 2 + x_lo), y: 4, z: 4, core: 2. Of those that a mesh axis runs over, the one named last changes fastest.
Arguments:
- loadings: float32 [64, 32, 16384], P(None, None, ('row', 'col')), may hold values from -6 to 6
Outputs:
- correlation: float32 [16384, 16384], P('row', 'col')
All inputs are finite; a program needn't handle non-finite values.
Results may differ from a plain program's by a relative error of at most 0.000096.
Values sent between devices are 32-bit elements; how exact they have to be, the bound alone decides.
No kernel may reach another device: no remote copies, remote signals or barrier semaphores. Data moves between devices by JAX's collectives and lax.ppermute only.
A program may use at most 128 MiB of HBM per device.

v0:
```python
import jax
import jax.numpy as jnp
from jax import lax
from jax.sharding import PartitionSpec as P


def padded_to(lines, devices):
    spare = -len(lines) % devices
    return jnp.pad(lines, [(0, spare)] + [(0, 0)] * (lines.ndim - 1))


def broadcast_by_parts(value, axis, root):
    lines = jnp.where(lax.axis_index(axis) == root, value, jnp.zeros_like(value)).reshape(
        -1, *value.shape[1:][-1:]
    )
    padded = padded_to(lines, lax.axis_size(axis))
    own = lax.psum_scatter(padded, axis, scatter_dimension=0, tiled=True)
    return lax.all_gather(own, axis, axis=0, tiled=True)[: len(lines)].reshape(value.shape)


def tile_product(left, right, count):
    depth = left.shape[0] * left.shape[1]
    flat_left = left.reshape(depth, left.shape[2])
    flat_right = right.reshape(depth, right.shape[2])
    total = lax.dot_general(
        flat_left,
        flat_right,
        (((0,), (0,)), ((), ())),
        precision=lax.Precision.HIGHEST,
        preferred_element_type=jnp.float32,
    )
    return total * (1.0 / count)


def column_source(group_block):
    halves = lax.axis_size("col") // lax.axis_size("row")
    width = group_block.shape[2] // halves
    position = lax.axis_index("col")
    start = position % halves * width
    candidate = lax.dynamic_slice_in_dim(group_block, start, width, 2)
    return broadcast_by_parts(candidate, "row", position // halves)


def local(loadings):
    count = loadings.shape[0]
    variance = jnp.sum(loadings * loadings, axis=1, keepdims=True)
    scaled = loadings / jnp.sqrt(variance)
    group_block = lax.all_gather(scaled, "col", axis=2, tiled=True)
    columns_block = column_source(group_block)
    return tile_product(lax.all_gather(scaled, "col", axis=2, tiled=True), columns_block, count)


def solution(mesh):
    placed = (P(None, None, ("row", "col")),)
    return jax.shard_map(
        local, mesh=mesh, in_specs=placed, out_specs=P("row", "col"), check_vma=False
    )
```

profile of v0, /device:TPU:1, one launch (start us, length us, event | category | flops | bytes accessed | tf_op | source)
XLA Modules:
  0.0 388.7 jit_solution(10311597832348095718)
XLA Ops:
  6.5 0.0 all-gather.3.cloned.1.call-start
  6.5 1.4 multiply_reduce_fusion
  8.0 2.3 broadcast_divide_fusion
  10.3 0.0 all-gather.3.cloned.1.call-update
  10.3 0.0 reduce-scatter.2.cloned.1.call-start
  10.4 121.7 %all-gather.3.cloned.1.call-done = f32[64,32,2048]{2,1,0:T(8,128)} async-done(((f32[64,32,128]{2,1,0:T(8,128)}), f32[64,32,2048]{2,1,0:T(8,128)}) %all-gather.3.cloned.1.call-update) | async-done | bytes 16777232 | tf_op jit(solution)/shard_map/all_gather | solution.py:50
  132.2 8.7 %dynamic-slice_select_fusion = f32[64,32,1024]{2,1,0:T(8,128)} fusion(f32[64,32,2048]{2,1,0:T(8,128)} %all-gather.3.cloned.1.call-done, s32[]{:T(128)S(6)} %select_n.25, pred[]{:T(512)S(6)} %eq.5), kind=kLoop, calls=%fused_computation | loop fusion | flops 2097152 | bytes 16777220 | tf_op jit(solution)/shard_map/jit(_where)/select_n | solution.py:13
  140.8 0.0 reduce-scatter.2.cloned.1.call-update
  140.9 0.0 all-gather.5.cloned.1.call-start
  140.9 89.8 %reduce-scatter.2.cloned.1.call-done = f32[256,1024]{1,0:T(8,128)} async-done(((f32[2048,1024]{1,0:T(8,128)}), f32[256,1024]{1,0:T(8,128)}) %reduce-scatter.2.cloned.1.call-update) | async-done | bytes 1048592 | tf_op jit(solution)/shard_map/reduce_scatter | solution.py:17
  230.7 0.0 all-gather.5.cloned.1.call-update
  230.7 92.3 %all-gather.5.cloned.1.call-done = f32[2048,1024]{1,0:T(8,128)} async-done(((f32[256,1024]{1,0:T(8,128)}), f32[2048,1024]{1,0:T(8,128)}) %all-gather.5.cloned.1.call-update) | async-done | bytes 8388624 | tf_op jit(solution)/shard_map/all_gather | solution.py:18
  323.0 59.2 %convolution_multiply_fusion = f32[2048,1024]{1,0:T(8,128)} fusion(f32[2048,2048]{1,0:T(8,128)} %bitcast.5, f32[2048,1024]{1,0:T(8,128)} %all-gather.5.cloned.1.call-done), kind=kOutput, calls=%fused_computation.1 | convolution fusion | flops 51541704704 | bytes 33554432 | tf_op jit(solution)/shard_map/dot_general | solution.py:25
  (1 shorter events, 0.0 us)
Async XLA Ops:
  6.5 125.6 %all-gather.3.cloned.1.call-start = ((), (), s32[]{:S(2)}) async-start(), calls=%async_computation.1 | async-start | bytes 17825792 | tf_op jit(solution)/shard_map/all_gather | solution.py:50
  10.3 220.4 %reduce-scatter.2.cloned.1.call-start = ((), (), s32[]{:S(2)}) async-start(), calls=%async_computation.2 | async-start | bytes 9437184 | tf_op jit(solution)/shard_map/reduce_scatter | solution.py:17
  140.9 182.2 %all-gather.5.cloned.1.call-start = ((), (), s32[]{:S(2)}) async-start(), calls=%async_computation.3 | async-start | bytes 9437184 | tf_op jit(solution)/shard_map/all_gather | solution.py:18
Sparse Core Ops, SparseCore 0:
  10.5 121.6 all-gather.2
  141.0 89.6 reduce-scatter.1
  232.4 90.6 all-gather.4
where the time goes:
time: 389 us
  waiting for transfers between devices  304 us (78%)
  matrix products  59.2 us (15%)
  between operations  13.1 us (3%)
  other arithmetic  12.4 us (3%)
    all_gather x1, waiting for transfers between devices, local(): lax.all_gather(scaled, 'col', axis=2, tiled=True)  122 us
    all_gather x1, waiting for transfers between devices, broadcast_by_parts(): lax.all_gather(own, axis, axis=0, tiled=True)[:len(lines)]  92.3 us
    reduce_scatter x1, waiting for transfers between devices, broadcast_by_parts(): own = lax.psum_scatter(padded, axis, scatter_dimension=0, tiled=True)  89.8 us
    dot_general x1, matrix products, tile_product(): lax.dot_general(flat_left, flat_right, (((0,), (0,)), ((), ())), precisio...  59.2 us
    select_n x1, other arithmetic, broadcast_by_parts(): jnp.where(lax.axis_index(axis) == root, value, jnp.zeros_like(value))  8.68 us
  transfers between devices with their start and end apart: 3, of which 3 were waited for; matrix products, arithmetic and copies ran while one was open for 0% of the time, Pallas kernels for 0%

commit v1 on v0

v1 whole, which is shorter than its diff:
```python
import jax
import jax.numpy as jnp
from jax import lax
from jax.sharding import PartitionSpec as P


def column_pairs(rows, cols):
    halves = cols // rows
    pairs = []
    for r in range(rows):
        for c in range(cols):
            pairs.append(((c // halves) * cols + (c % halves) * rows + r, r * cols + c))
    return pairs


def local(loadings):
    count, factors, width = loadings.shape
    depth = count * factors
    variance = jnp.sum(loadings * loadings, axis=1, keepdims=True)
    scaled = loadings / jnp.sqrt(variance)
    pairs = column_pairs(lax.axis_size("row"), lax.axis_size("col"))
    moved = lax.ppermute(scaled, ("row", "col"), pairs)
    right = lax.all_gather(moved, "row", axis=2, tiled=True)
    left = lax.all_gather(scaled, "col", axis=2, tiled=True)
    total = lax.dot_general(
        left.reshape(depth, -1),
        right.reshape(depth, -1),
        (((0,), (0,)), ((), ())),
        precision=lax.Precision.HIGH,
        preferred_element_type=jnp.float32,
    )
    return total * (1.0 / count)


def solution(mesh):
    placed = (P(None, None, ("row", "col")),)
    return jax.shard_map(
        local, mesh=mesh, in_specs=placed, out_specs=P("row", "col"), check_vma=False
    )
```

time: 389 us -> 369 us (0.949)
  matrix products: 59.2 us -> 33.4 us
  other arithmetic: 12.4 us -> 3.26 us
  waiting for transfers between devices: 304 us -> 312 us
  starting transfers between devices: 0.09 us -> 4.97 us
    reduce_scatter x1 -> x0, waiting for transfers between devices: 89.8 us -> none  [broadcast_by_parts(): own = lax.psum_scatter(padded, axis, scatter_dimension=0, tiled=True)]
    all_gather x2, waiting for transfers between devices: 214 us -> 270 us  [the longest x1 146 us: local(): right = lax.all_gather(moved, 'row', axis=2, tiled=True)]
    ppermute x0 -> x1, waiting for transfers between devices: none -> 41.8 us  [local(): moved = lax.ppermute(scaled, ('row', 'col'), pairs)]
    dot_general x1, matrix products: 59.2 us -> 33.4 us  [local(): lax.dot_general(left.reshape(depth, -1), right.reshape(depth, -1), (((0,)...]
    select_n x1 -> x0, other arithmetic: 8.68 us -> none  [broadcast_by_parts(): jnp.where(lax.axis_index(axis) == root, value, jnp.zeros_like(value))]
    ppermute x0 -> x1, starting transfers between devices: none -> 4.92 us  [local(): moved = lax.ppermute(scaled, ('row', 'col'), pairs)]
where the time goes in v1:
time: 369 us; the launch traced here: 368 us
  waiting for transfers between devices  312 us (85%)
  matrix products  33.4 us (9%)
  between operations  13.4 us (4%)
  starting transfers between devices  4.97 us (1%)
    all_gather x1, waiting for transfers between devices, local(): right = lax.all_gather(moved, 'row', axis=2, tiled=True)  146 us
    all_gather x1, waiting for transfers between devices, local(): left = lax.all_gather(scaled, 'col', axis=2, tiled=True)  124 us
    ppermute x1, waiting for transfers between devices, local(): moved = lax.ppermute(scaled, ('row', 'col'), pairs)  41.8 us
    dot_general x1, matrix products, local(): lax.dot_general(left.reshape(depth, -1), right.reshape(depth, -1), (((0,)...  33.4 us
  transfers between devices with their start and end apart: 3, of which 3 were waited for; matrix products, arithmetic and copies ran while one was open for 0% of the time, Pallas kernels for 0%

profile of v1, /device:TPU:1, one launch (start us, length us, event | category | flops | bytes accessed | tf_op | source)
XLA Modules:
  0.0 368.4 jit_solution(17586904733066292045)
XLA Ops:
  6.5 0.0 all-gather.5.cloned.1.call-start
  6.5 1.4 multiply_reduce_fusion
  8.0 1.8 copy_divide_fusion
  9.8 0.0 copy-start
  9.8 4.9 %collective-permute-start = (f32[64,32,128]{2,0,1:T(8,128)S(1)}, f32[64,32,128]{2,0,1:T(8,128)S(1)}, u32[]{:S(2)}, u32[]{:S(2)}) collective-permute-start(f32[64,32,128]{2,0,1:T(8,128)S(1)} %copy_divide_fusion), channel_id=1, source_target_pairs={{0,0},{8,1},{16,2},{24,3},{32,4},{40,5},{48,6},{56,7},{64,8},{72,9... | collective-permute-start | bytes 3145736 | tf_op jit(solution)/shard_map/ppermute | solution.py:22
  14.8 41.8 %collective-permute-done = f32[64,32,128]{2,0,1:T(8,128)S(1)} collective-permute-done((f32[64,32,128]{2,0,1:T(8,128)S(1)}, f32[64,32,128]{2,0,1:T(8,128)S(1)}, u32[]{:S(2)}, u32[]{:S(2)}) %collective-permute-start) | collective-permute-done | bytes 1048608 | tf_op jit(solution)/shard_map/ppermute | solution.py:22
  56.6 0.0 copy-start.1
  56.6 1.0 copy-done.1
  57.7 0.0 all-gather.5.cloned.1.call-update
  57.7 0.0 all-gather.3.cloned.1.call-start
  57.7 0.0 copy-done
  57.8 0.7 all-gather.3.cloned.1.call-update
  58.4 145.7 %all-gather.5.cloned.1.call-done = f32[64,32,1024]{2,0,1:T(8,128)} async-done(((f32[64,32,128]{2,0,1:T(8,128)}), f32[64,32,1024]{2,0,1:T(8,128)}) %all-gather.5.cloned.1.call-update) | async-done | bytes 8388624 | tf_op jit(solution)/shard_map/all_gather | solution.py:23
  204.1 124.0 %all-gather.3.cloned.1.call-done = f32[64,32,2048]{2,0,1:T(8,128)} async-done(((f32[64,32,128]{2,0,1:T(8,128)}), f32[64,32,2048]{2,0,1:T(8,128)}) %all-gather.3.cloned.1.call-update) | async-done | bytes 16777232 | tf_op jit(solution)/shard_map/all_gather | solution.py:24
  328.1 33.4 %bitcast_multiply_fusion = f32[2048,1024]{1,0:T(8,128)} fusion(f32[64,32,2048]{2,0,1:T(8,128)} %all-gather.3.cloned.1.call-done, f32[64,32,1024]{2,0,1:T(8,128)} %all-gather.5.cloned.1.call-done), kind=kOutput, calls=%fused_computation | convolution fusion | flops 25771900928 | bytes 33554432 | tf_op jit(solution)/shard_map/dot_general | solution.py:25
  (1 shorter events, 0.0 us)
Async XLA Ops:
  6.5 197.6 %all-gather.5.cloned.1.call-start = ((), (), s32[]{:S(2)}) async-start(), calls=%async_computation.1 | async-start | bytes 9437184 | tf_op jit(solution)/shard_map/all_gather | solution.py:23
  9.8 47.9 %copy-start = (f32[64,32,128]{2,0,1:T(8,128)}, f32[64,32,128]{2,0,1:T(8,128)S(1)}, u32[]{:S(2)}) copy-start(f32[64,32,128]{2,0,1:T(8,128)S(1)} %copy_divide_fusion) | copy-start | bytes 3145732
  9.8 46.8 %collective-permute-start = (f32[64,32,128]{2,0,1:T(8,128)S(1)}, f32[64,32,128]{2,0,1:T(8,128)S(1)}, u32[]{:S(2)}, u32[]{:S(2)}) collective-permute-start(f32[64,32,128]{2,0,1:T(8,128)S(1)} %copy_divide_fusion), channel_id=1, source_target_pairs={{0,0},{8,1},{16,2},{24,3},{32,4},{40,5},{48,6},{56,7},{64,8},{72,9... | collective-permute-start | bytes 3145736 | tf_op jit(solution)/shard_map/ppermute | solution.py:22
  56.6 1.1 copy-start.1
  57.7 270.4 %all-gather.3.cloned.1.call-start = ((), (), s32[]{:S(2)}) async-start(), calls=%async_computation | async-start | bytes 17825792 | tf_op jit(solution)/shard_map/all_gather | solution.py:24
Sparse Core Ops, SparseCore 0:
  57.8 146.2 all-gather.4
  206.4 121.6 all-gather.2
